TPU v7x, 32 devices: a whole 2x2x4 slice. The times are simulated.
32 devices in a mesh: patch: 8 (over y, x, core), rhs: 4 (over z).
Axes of the slice: x: 2, y: 2, z: 4, core: 2. Of those that a mesh axis runs over, the one named last changes fastest.
Arguments:
- rhs_vectors: float32 [64, 16, 384], P('patch', 'rhs'), may hold values from -8 to 8
- near_blocks: bfloat16 [64, 4, 384, 384], P('patch'), may hold values from -1 to 5, as said below
- neighbours: int32 [64, 4], P('patch'), may hold values from 0 to 63, as said below
- up_maps: float32 [64, 64, 384], P('patch'), may hold values from -0.3125 to 0.3125
- shift_up: float32 [64, 64, 64], P('patch'), may hold values from -0.25 to 0.25
- far_lists: int32 [8, 4], P('patch'), may hold values from 0 to 7, as said below
- translations: float32 [8, 4, 64, 64], P('patch'), may hold values from -0.375 to 0.375
- shift_down: float32 [64, 64, 64], P('patch'), may hold values from -0.75 to 0.75
- down_maps: float32 [64, 384, 64], P('patch'), may hold values from -0.375 to 0.375
Outputs:
- solution: float32 [64, 16, 384], P('patch', 'rhs')
- residual: float32 [64, 16, 384], P('patch', 'rhs')
Inputs may be any that keep to these rules, and one draw needn't show every extreme that they name: `neighbours`: entry 0 of each row is the patch itself; every other entry names a patch of the same cell or of the cell just before or just after it, cyclically. `far_lists`: entry 0 of each row names the cell just before or just after the row's own cell, cyclically, and for cell 0 the cell just before it; every other entry names a cell other than the row's own. `near_blocks`: the blocks keep the operator's symmetric part positive definite.
All inputs are finite; a program needn't handle non-finite values.
Results may differ from a plain program's by a relative error of at most 0.008.
The roundings to bfloat16 on the way count: a program that leaves them out, or rounds other values in their place, can miss the bound.
Values may be sent and summed in bfloat16 or wider, within the bound.
A program may use at most 64 MiB of HBM per device.

v0:
```python
import jax
import jax.numpy as jnp
from jax import lax
from jax.sharding import PartitionSpec as P

ITERS = 2


HIGH = lax.Precision.HIGHEST


def with_halo(block, sides, width):
    for axis, dim in sides:
        count = lax.axis_size(axis)
        forward = [(i, i + 1) for i in range(count - 1)]
        forward.append((count - 1, 0))
        backward = [(target, source) for source, target in forward]
        low = lax.ppermute(
            lax.slice_in_dim(block, block.shape[dim] - width, None, axis=dim), axis, forward
        )
        high = lax.ppermute(lax.slice_in_dim(block, 0, width, axis=dim), axis, backward)
        block = jnp.concatenate([low, block, high], axis=dim)
    return block


def spd_solve(matrix, right):
    factor = jnp.linalg.cholesky(matrix)
    return jax.scipy.linalg.cho_solve((factor, True), right)


def gram(left, right):
    return jnp.einsum("pkw,plw->kl", left, right, precision=HIGH)


def mix(field, coeffs):
    return jnp.einsum("pkw,kl->plw", field, coeffs, precision=HIGH)


def residual_sum(residual):
    return lax.psum(gram(residual, residual), "patch")


def apply_operator(
    field,
    near_blocks,
    neighbours,
    up_maps,
    shift_up,
    far_lists,
    translations,
    shift_down,
    down_maps,
):
    patches = field.shape[0]
    count = lax.axis_size("patch")
    first = lax.axis_index("patch") * patches - patches
    rounded = field.astype(jnp.bfloat16)
    widened = with_halo(rounded, (("patch", 0),), patches)
    local_ids = jnp.mod(neighbours - first, patches * count)
    picked = widened[local_ids]
    near = jnp.einsum("pjvw,pjkw->pkv", near_blocks, picked, preferred_element_type=jnp.float32)
    moments = jnp.einsum("pew,pkw->pke", up_maps, field, precision=HIGH)
    cell_moment = jnp.einsum("pfe,pke->kf", shift_up, moments, precision=HIGH)
    sources = far_lists[0]
    table = translations[0]
    piece = lax.all_gather(cell_moment[None], "patch", axis=0, tiled=True)
    labels = jnp.arange(piece.shape[0], dtype=jnp.int32)
    select = (sources[:, None] == labels[None, :]).astype(jnp.float32)
    chosen = jnp.einsum("ji,ike->jke", select, piece, precision=HIGH)
    local_exp = jnp.zeros_like(cell_moment) + jnp.einsum(
        "jfe,jke->kf", table, chosen, precision=HIGH
    )
    patch_exp = jnp.einsum("pfe,ke->pkf", shift_down, local_exp, precision=HIGH)
    far = jnp.einsum("pvf,pkf->pkv", down_maps, patch_exp, precision=HIGH)
    return near + far


def on_device(
    rhs_vectors,
    near_blocks,
    neighbours,
    up_maps,
    shift_up,
    far_lists,
    translations,
    shift_down,
    down_maps,
):
    my_cols = rhs_vectors.shape[1]
    offset = lax.axis_index("rhs") * my_cols
    residual = lax.all_gather(rhs_vectors, "rhs", axis=1, tiled=True)
    solution = jnp.zeros_like(residual)
    direction = residual
    current = jnp.zeros((residual.shape[1], residual.shape[1]), jnp.float32)
    for step in range(ITERS):
        image = apply_operator(
            direction,
            near_blocks,
            neighbours,
            up_maps,
            shift_up,
            far_lists,
            translations,
            shift_down,
            down_maps,
        )
        if step == 0:
            current = residual_sum(residual)
        curve = lax.psum(gram(direction, image), "patch")
        curve = 0.5 * (curve + curve.T)
        alpha = spd_solve(curve, current)
        solution = solution + mix(direction, alpha)
        residual = residual - mix(image, alpha)
        if step + 1 < ITERS:
            following = residual_sum(residual)
            beta = spd_solve(current, following)
            direction = residual + mix(direction, beta)
            current = following
    solution_mine = lax.dynamic_slice_in_dim(solution, offset, my_cols, 1)
    residual_mine = lax.dynamic_slice_in_dim(residual, offset, my_cols, 1)
    return (solution_mine, residual_mine)


def solution(mesh):
    return jax.shard_map(
        on_device,
        mesh=mesh,
        in_specs=(
            P("patch", "rhs", None),
            P("patch", None, None, None),
            P("patch", None),
            P("patch", None, None),
            P("patch", None, None),
            P("patch", None),
            P("patch", None, None, None),
            P("patch", None, None),
            P("patch", None, None),
        ),
        out_specs=(P("patch", "rhs", None), P("patch", "rhs", None)),
        check_vma=False,
    )
```

profile of v0, /device:TPU:0, one launch (start us, length us, event | category | flops | bytes accessed | tf_op | source)
XLA Modules:
  0.0 129.5 jit_solution(5300560113778208520)
XLA Ops:
  0.6 0.9 copy.61
  1.5 15.5 %all_gather.9 = f32[8,16,384]{2,0,1:T(8,128)S(1)} all-gather(f32[8,4,384]{2,0,1:T(8,128)S(1)} %copy.61), channel_id=1, replica_groups=mesh['patch'=8,'rhs'=4] {'rhs'}, dimensions={1}, use_global_device_ids=true | all-gather | bytes 245760 | tf_op jit(solution)/shard_map/all_gather | solution.py:91
  17.1 0.5 collective-permute-start
  17.6 0.4 convolution_bitcast_fusion.14
  17.9 0.7 compare_select_fusion
  18.8 2.1 %fusion.11 = f32[8,16,64]{2,1,0:T(8,128)S(1)} fusion(f32[8,64,384]{2,1,0:T(8,128)} %param.15, f32[8,16,384]{2,0,1:T(8,128)S(1)} %all_gather.9), kind=kOutput, calls=%fused_computation.33 | convolution fusion | flops 37748736 | bytes 1015808 | tf_op jit(solution)/shard_map/pew,pkw->pke/dot_general | solution.py:62
  20.9 1.2 convolution_bitcast_fusion.11
  22.1 9.3 %all-gather = f32[128,64]{1,0:T(8,128)S(1)} all-gather(f32[16,64]{1,0:T(8,128)S(1)} %convolution_bitcast_fusion.11), channel_id=2, replica_groups=mesh['patch'=8,'rhs'=4] {'patch'}, dimensions={0}, use_global_device_ids=true | all-gather | bytes 36864 | tf_op jit(solution)/shard_map/all_gather | solution.py:66
  31.4 0.9 fusion.15
  32.3 1.1 fusion.4
  33.4 1.7 %convolution_bitcast_fusion.6 = f32[8,16,64]{2,1,0:T(8,128)S(1)} fusion(f32[16,64,1]{1,0,2:T(8,128)S(1)} %fusion.4, f32[8,64,64]{2,1,0:T(8,128)} %param.19), kind=kOutput, calls=%fused_computation.12 | convolution fusion | flops 6291456 | bytes 167936 | tf_op jit(solution)/shard_map/pfe,ke->pkf/dot_general | solution.py:73
  35.2 0.6 gather_fusion
  35.9 6.3 %convolution_bitcast_fusion.4 = f32[8,16,384]{2,1,0:T(8,128)S(1)} fusion(bf16[8,4,16,384]{3,2,1,0:T(8,128)(2,1)S(1)} %bitcast.140, bf16[8,4,384,384]{3,2,1,0:T(8,128)(2,1)} %param.13), kind=kOutput, calls=%fused_computation.10 | convolution fusion | flops 150994944 | bytes 10027008 | tf_op jit(solution)/shard_map/pjvw,pjkw->pkv/dot_general | solution.py:61
  42.2 0.6 convolution_add_fusion.1
  42.8 0.4 convolution_bitcast_fusion.15
  43.2 23.6 %all-reduce = (f32[16,16]{0,1:T(8,128)S(1)}, f32[16,16]{1,0:T(8,128)S(1)}) all-reduce(f32[16,16]{0,1:T(8,128)S(1)} %convolution_bitcast_fusion.14, f32[16,16]{1,0:T(8,128)S(1)} %convolution_bitcast_fusion.15), channel_id=1, replica_groups=mesh['patch'=8,'rhs'=4] {'patch'}, use_global_device_ids=true, to_apply=%region_3.5 | all-reduce | flops 512 | bytes 4096 | tf_op jit(solution)/shard_map/psum | solution.py:40
  67.0 1.5 %cholesky.59 = f32[16,16]{1,0:T(8,128)S(1)} custom-call(f32[16,16]{1,0:T(8,128)S(1)} %fusion.35), custom_call_target="Cholesky" | custom-call | tf_op jit(solution)/shard_map/jit(cholesky)/cholesky | solution.py:27
  68.4 0.6 compare_reduce_fusion.2
  69.1 0.6 fusion.20
  69.8 1.2 custom-call.9
  71.5 0.3 fusion.1
  71.8 0.3 convolution_bitcast_fusion.13
  72.1 12.1 %psum.30 = f32[16,16]{1,0:T(8,128)S(1)} all-reduce(f32[16,16]{1,0:T(8,128)S(1)} %convolution_bitcast_fusion.13), channel_id=1, replica_groups=mesh['patch'=8,'rhs'=4] {'patch'}, use_global_device_ids=true, to_apply=%region_4.7 | all-reduce | flops 256 | bytes 2048 | tf_op jit(solution)/shard_map/psum | solution.py:40
  84.2 1.4 %cholesky.70 = f32[16,16]{1,0:T(8,128)S(1)} custom-call(f32[16,16]{1,0:T(8,128)S(1)} %fusion.31), custom_call_target="Cholesky" | custom-call | tf_op jit(solution)/shard_map/jit(cholesky)/cholesky | solution.py:27
  85.7 0.6 compare_reduce_fusion.1
  86.3 0.6 fusion.21
  87.0 1.2 custom-call.10
  88.6 0.3 fusion.43
  89.0 0.5 collective-permute-start.2
  89.5 0.3 fusion.7
  89.8 0.9 fusion.44
  90.8 0.3 convolution_bitcast_fusion.8
  91.1 9.4 %all-gather.1 = f32[128,64]{1,0:T(8,128)S(1)} all-gather(f32[16,64]{1,0:T(8,128)S(1)} %convolution_bitcast_fusion.8), channel_id=3, replica_groups=mesh['patch'=8,'rhs'=4] {'patch'}, dimensions={0}, use_global_device_ids=true | all-gather | bytes 36864 | tf_op jit(solution)/shard_map/all_gather | solution.py:66
  100.4 0.2 fusion.13
  100.9 0.7 convolution_bitcast_fusion.5
  101.7 0.6 gather_fusion.1
  102.3 6.2 %convolution_bitcast_fusion.3 = f32[8,16,384]{2,1,0:T(8,128)S(1)} fusion(bf16[8,4,16,384]{3,2,1,0:T(8,128)(2,1)S(1)} %bitcast.139, bf16[8,4,384,384]{3,2,1,0:T(8,128)(2,1)} %param.13), kind=kOutput, calls=%fused_computation.9 | convolution fusion | flops 150994944 | bytes 10027008 | tf_op jit(solution)/shard_map/pjvw,pjkw->pkv/dot_general | solution.py:61
  108.5 0.6 convolution_add_fusion
  109.2 0.3 convolution_bitcast_fusion.12
  109.5 13.5 %psum.31 = f32[16,16]{1,0:T(8,128)S(1)} all-reduce(f32[16,16]{1,0:T(8,128)S(1)} %convolution_bitcast_fusion.12), channel_id=1, replica_groups=mesh['patch'=8,'rhs'=4] {'patch'}, use_global_device_ids=true, to_apply=%region_5.8 | all-reduce | flops 256 | bytes 2048 | tf_op jit(solution)/shard_map/psum | solution.py:109
  123.1 1.5 %cholesky.81 = f32[16,16]{1,0:T(8,128)S(1)} custom-call(f32[16,16]{1,0:T(8,128)S(1)} %fusion.26), custom_call_target="Cholesky" | custom-call | tf_op jit(solution)/shard_map/jit(cholesky)/cholesky | solution.py:27
  124.6 0.6 compare_reduce_fusion
  125.3 0.6 fusion.22
  125.9 1.2 custom-call.11
  127.6 0.3 fusion.45
  127.9 0.3 convolution_bitcast_fusion
  128.2 0.6 dynamic-slice_subtract_fusion
  128.8 0.6 fusion.17
  (44 shorter events, 2.4 us)
Async XLA Ops:
  0.6 41.6 %copy-start = (f32[8,384,64]{1,2,0:T(8,128)S(1)}, f32[8,384,64]{1,2,0:T(8,128)}, u32[]{:S(2)}) copy-start(f32[8,384,64]{1,2,0:T(8,128)} %param.20) | copy-start | bytes 2359300
  17.0 18.1 %collective-permute-start.1 = (bf16[8,16,384]{2,1,0:T(8,128)(2,1)S(1)}, bf16[8,16,384]{2,1,0:T(8,128)(2,1)S(1)}, u32[]{:S(2)}, u32[]{:S(2)}) collective-permute-start(bf16[8,16,384]{2,1,0:T(8,128)(2,1)S(1)} %copy.116), channel_id=1, source_target_pairs={{4,0},{8,4},{12,8},{16,12},{20,16},{24,20},{28,24},{0,28},{5,1},{9... | collective-permute-start | bytes 294920 | tf_op jit(solution)/shard_map/ppermute | solution.py:21
  17.1 18.1 %collective-permute-start = (bf16[8,16,384]{2,1,0:T(8,128)(2,1)S(1)}, bf16[8,16,384]{2,1,0:T(8,128)(2,1)S(1)}, u32[]{:S(2)}, u32[]{:S(2)}) collective-permute-start(bf16[8,16,384]{2,1,0:T(8,128)(2,1)S(1)} %copy.116), channel_id=1, source_target_pairs={{0,4},{4,8},{8,12},{12,16},{16,20},{20,24},{24,28},{28,0},{1,5},{5... | collective-permute-start | bytes 294920 | tf_op jit(solution)/shard_map/ppermute | solution.py:18
  35.8 54.0 %copy-start.1 = (f32[8,64,384]{2,1,0:T(8,128)S(1)}, f32[8,64,384]{2,1,0:T(8,128)}, u32[]{:S(2)}) copy-start(f32[8,64,384]{2,1,0:T(8,128)} %param.15) | copy-start | bytes 2359300
  35.8 54.9 %copy-start.2 = (f32[8,64,64]{2,1,0:T(8,128)S(1)}, f32[8,64,64]{2,1,0:T(8,128)}, u32[]{:S(2)}) copy-start(f32[8,64,64]{2,1,0:T(8,128)} %param.16) | copy-start | bytes 393220
  35.9 64.6 %copy-start.5 = (s32[1,4]{1,0:T(1,128)S(1)}, s32[1,4]{1,0:T(1,128)}, u32[]{:S(2)}) copy-start(s32[1,4]{1,0:T(1,128)} %param.17) | copy-start | bytes 52
  35.9 64.8 %copy-start.4 = (f32[1,4,64,64]{3,2,1,0:T(8,128)S(1)}, f32[1,4,64,64]{3,2,1,0:T(8,128)}, u32[]{:S(2)}) copy-start(f32[1,4,64,64]{3,2,1,0:T(8,128)} %param.18) | copy-start | bytes 196612
  35.9 65.0 %copy-start.3 = (f32[8,64,64]{2,1,0:T(8,128)S(1)}, f32[8,64,64]{2,1,0:T(8,128)}, u32[]{:S(2)}) copy-start(f32[8,64,64]{2,1,0:T(8,128)} %param.19) | copy-start | bytes 393220
  89.0 12.6 %collective-permute-start.3 = (bf16[8,16,384]{2,1,0:T(8,128)(2,1)S(1)}, bf16[8,16,384]{2,1,0:T(8,128)(2,1)S(1)}, u32[]{:S(2)}, u32[]{:S(2)}) collective-permute-start(bf16[8,16,384]{2,1,0:T(8,128)(2,1)S(1)} %get-tuple-element.6), channel_id=1, source_target_pairs={{4,0},{8,4},{12,8},{16,12},{20,16},{24,20},{28,24},{0,28},{5,1},{9... | collective-permute-start | bytes 294920 | tf_op jit(solution)/shard_map/ppermute | solution.py:21
  89.0 12.6 %collective-permute-start.2 = (bf16[8,16,384]{2,1,0:T(8,128)(2,1)S(1)}, bf16[8,16,384]{2,1,0:T(8,128)(2,1)S(1)}, u32[]{:S(2)}, u32[]{:S(2)}) collective-permute-start(bf16[8,16,384]{2,1,0:T(8,128)(2,1)S(1)} %get-tuple-element.6), channel_id=1, source_target_pairs={{0,4},{4,8},{8,12},{12,16},{16,20},{20,24},{24,28},{28,0},{1,5},{5... | collective-permute-start | bytes 294920 | tf_op jit(solution)/shard_map/ppermute | solution.py:18
where the time goes:
time: 130 us; the launch traced here: 129 us
  blocking collectives  83.3 us (64%)
  matrix products  27.2 us (21%)
  other arithmetic  14.2 us (11%)
  local copies, waits for them, and re-layouts  2.76 us (2%)
    psum x2, blocking collectives, residual_sum(): return lax.psum(gram(residual, residual), 'patch')  35.7 us
    all_gather x2, blocking collectives, apply_operator(): piece = lax.all_gather(cell_moment[None], 'patch', axis=0, tiled=True)  18.7 us
    all_gather x1, blocking collectives, on_device(): residual = lax.all_gather(rhs_vectors, 'rhs', axis=1, tiled=True)  15.5 us
    psum x1, blocking collectives, on_device(): curve = lax.psum(gram(direction, image), 'patch')  13.5 us
    dot_general x2, matrix products, apply_operator(): jnp.einsum('pjvw,pjkw->pkv', near_blocks, picked, preferred_element_type=...  12.5 us
    another operation x9, other arithmetic, spd_solve(): factor = jnp.linalg.cholesky(matrix)  6.39 us
    another operation x6, other arithmetic, spd_solve(): return jax.scipy.linalg.cho_solve((factor, True), right)  5.63 us
    dot_general x2, matrix products, apply_operator(): moments = jnp.einsum('pew,pkw->pke', up_maps, field, precision=HIGH)  2.99 us
  transfers between devices with their start and end apart: 4, of which 0 were waited for; matrix products, arithmetic and copies ran while one was open for 8% of the time, Pallas kernels for 0%

commit v1 on v0

v1 whole, which is shorter than its diff:
```python
import functools

import jax
import jax.numpy as jnp
from jax import lax
from jax.experimental import pallas as pl
from jax.experimental.pallas import tpu as pltpu
from jax.sharding import PartitionSpec as P

ITERS = 2
HIGH = lax.Precision.HIGHEST
MESH = pl.DeviceIdType.MESH


def nt(a, b, precision=HIGH):
    return lax.dot_general(
        a, b, (((1,), (1,)), ((), ())), precision=precision, preferred_element_type=jnp.float32
    )


def nn(a, b):
    return lax.dot_general(
        a, b, (((1,), (0,)), ((), ())), precision=HIGH, preferred_element_type=jnp.float32
    )


def eliminate(systems):
    n = systems[0].shape[0]
    for k in range(n):
        done = []
        for a in systems:
            rows = lax.broadcasted_iota(jnp.int32, a.shape, 0)
            row = a[k : k + 1, :] / a[k : k + 1, k : k + 1]
            done.append(jnp.where(rows == k, row, a - a[:, k : k + 1] * row))
        systems = done
    return systems


def kernel(
    cells,
    zs,
    rhs,
    near_hbm,
    neigh,
    up_hbm,
    su_hbm,
    far,
    tr_hbm,
    sd_hbm,
    dn_hbm,
    sol_out,
    res_out,
    blocks,
    up,
    su,
    tr,
    sd,
    dn,
    halo,
    moment,
    mom_out,
    own_dir,
    own_img,
    own_res,
    gathered,
    images,
    full_r,
    full_i,
    full_d,
    strip_out,
    strips,
    new_out,
    news,
    near_sem,
    map_sem,
    halo_s,
    halo_r,
    mom_s,
    mom_r,
    gat_s,
    gat_r,
    img_s,
    img_r,
    strip_s,
    strip_r,
    new_s,
    new_r,
):
    c = lax.axis_index("patch")
    z = lax.axis_index("rhs")
    patches, cols, width = rhs.shape
    terms = su.shape[1]
    total_cols = cols * zs
    total = patches * cells
    devices = cells * zs
    me = c * zs + z

    maps = [(up_hbm, up), (su_hbm, su), (sd_hbm, sd), (dn_hbm, dn), (tr_hbm, tr)]
    map_copies = [
        pltpu.make_async_copy(src, dst, map_sem.at[i]) for i, (src, dst) in enumerate(maps)
    ]
    for copy in map_copies[:2]:
        copy.start()

    barrier = pltpu.get_barrier_semaphore()

    def greet(i, carry):
        other = lax.rem(me + i, devices)
        pl.semaphore_signal(
            barrier, inc=1, device_id=(other // zs, lax.rem(other, zs)), device_id_type=MESH
        )
        return carry

    lax.fori_loop(1, devices, greet, 0)

    def near_copy(p):
        return pltpu.make_async_copy(near_hbm.at[p], blocks.at[p], near_sem.at[p])

    def start_near(p, carry):
        near_copy(p).start()
        return carry

    lax.fori_loop(0, patches, start_near, 0)
    for copy in map_copies[2:]:
        copy.start()

    def cell_of(i):
        return lax.rem(c + i, cells)

    def halo_copy(it, src, side):
        target = cell_of(1 if side == 0 else cells - 1)
        dst = halo.at[it, pl.ds(0 if side == 0 else 2 * patches, patches)]
        return pltpu.make_async_remote_copy(
            src_ref=src,
            dst_ref=dst,
            send_sem=halo_s.at[it, side],
            recv_sem=halo_r.at[it, side],
            device_id=(target, z),
            device_id_type=MESH,
        )

    def moment_copy(it, target, slot):
        return pltpu.make_async_remote_copy(
            src_ref=mom_out.at[it],
            dst_ref=moment.at[it, slot],
            send_sem=mom_s.at[it, target],
            recv_sem=mom_r.at[it, slot],
            device_id=(target, z),
            device_id_type=MESH,
        )

    def z_copy(src, buf, ssem, rsem, target, slot):
        return pltpu.make_async_remote_copy(
            src_ref=src,
            dst_ref=buf.at[slot],
            send_sem=ssem.at[target],
            recv_sem=rsem.at[slot],
            device_id=(c, target),
            device_id_type=MESH,
        )

    def strip_copy(it, target, slot):
        return pltpu.make_async_remote_copy(
            src_ref=strip_out.at[it],
            dst_ref=strips.at[it, slot],
            send_sem=strip_s.at[it, target],
            recv_sem=strip_r.at[it, slot],
            device_id=(target // zs, lax.rem(target, zs)),
            device_id_type=MESH,
        )

    def new_copy(target, slot):
        return pltpu.make_async_remote_copy(
            src_ref=new_out,
            dst_ref=news.at[slot],
            send_sem=new_s.at[target],
            recv_sem=new_r.at[slot],
            device_id=(target, z),
            device_id_type=MESH,
        )

    def others(count, mine, body):
        def step(i, carry):
            body(lax.rem(mine + i, count))
            return carry

        lax.fori_loop(1, count, step, 0)

    def cell_moment(it, src):
        acc = jnp.zeros((cols, terms), jnp.float32)
        for p in range(patches):
            acc = acc + nt(nt(src[p], up[p]), su[p])
        mom_out[it, :, :] = jnp.zeros(mom_out.shape[1:], jnp.float32)
        mom_out[it, :, 0:terms] = acc

    def apply_operator(it):
        halo_copy(it, own_dir, 0).wait_recv()
        halo_copy(it, own_dir, 1).wait_recv()
        first = c * patches - patches

        def near(p, carry):
            if it == 0:
                near_copy(p).wait()
            acc = jnp.zeros((cols, width), jnp.float32)
            for j in range(neigh.shape[1]):
                if j == 0:
                    x = halo[it, patches + p]
                else:
                    spot = jnp.minimum(lax.rem(neigh[p, j] - first + total, total), 3 * patches - 1)
                    x = halo[it, spot]
                acc = acc + nt(x.astype(jnp.bfloat16), blocks[p, j], None)
            own_img[it, p] = acc
            return carry

        lax.fori_loop(0, patches, near, 0)
        others(cells, c, lambda s: moment_copy(it, s, s).wait_recv())
        if it == 0:
            for copy in map_copies[2:]:
                copy.wait()
        local = jnp.zeros((cols, terms), jnp.float32)
        for j in range(far.shape[1]):
            local = local + nt(moment[it, far[0, j]][:, 0:terms], tr[0, j])
        for p in range(patches):
            own_img[it, p] += nt(nt(local, sd[p]), dn[p])

    def assemble(full, buf):
        for p in range(patches):
            for s in range(zs):
                full[p, s * cols : (s + 1) * cols, :] = buf[s, p]

    map_copies[0].wait()
    map_copies[1].wait()
    cell_moment(0, rhs)
    halo[0, pl.ds(patches, patches)] = rhs[...]
    gathered[z] = rhs[...]
    pl.semaphore_wait(barrier, devices - 1)
    halo_copy(0, rhs, 0).start()
    halo_copy(0, rhs, 1).start()
    others(cells, c, lambda t: moment_copy(0, t, c).start())
    others(zs, z, lambda t: z_copy(rhs, gathered, gat_s, gat_r, t, z).start())

    sel = (
        lax.broadcasted_iota(jnp.int32, (cols, total_cols), 1)
        == lax.broadcasted_iota(jnp.int32, (cols, total_cols), 0) + z * cols
    ).astype(jnp.float32)
    eye = (
        lax.broadcasted_iota(jnp.int32, (total_cols, total_cols), 1)
        == lax.broadcasted_iota(jnp.int32, (total_cols, total_cols), 0)
    ).astype(jnp.float32)

    def share_strips(it, direction, with_rr):
        acc = jnp.zeros((cols, total_cols), jnp.float32)
        cur = jnp.zeros((cols, total_cols), jnp.float32)
        for p in range(patches):
            acc = acc + nt(own_img[it, p], direction[p])
            if with_rr:
                cur = cur + nt(rhs[p], direction[p])
        strip_out[it, 0, :, 0:total_cols] = acc
        strip_out[it, 1, :, 0:total_cols] = cur
        strips[it, me] = strip_out[it]
        others(devices, me, lambda t: strip_copy(it, t, me).start())

    def collect_strips(it):
        others(devices, me, lambda s: strip_copy(it, s, s).wait_recv())
        curve, cur = [], []
        for s in range(zs):
            acc = strips[it, s]
            for k in range(1, cells):
                acc = acc + strips[it, k * zs + s]
            curve.append(acc[0, :, 0:total_cols])
            cur.append(acc[1, :, 0:total_cols])
        curve = jnp.concatenate(curve, axis=0)
        cur = jnp.concatenate(cur, axis=0)
        return 0.5 * (curve + nt(eye, curve)), cur

    apply_operator(0)
    others(zs, z, lambda t: z_copy(own_img.at[0], images.at[0], img_s.at[0], img_r.at[0], t, z).start())
    images[0, z] = own_img[0]
    others(zs, z, lambda s: z_copy(rhs, gathered, gat_s, gat_r, s, s).wait_recv())
    assemble(full_r, gathered)
    share_strips(0, full_r, True)
    curve, current = collect_strips(0)
    solved, inverse = eliminate(
        [jnp.concatenate([curve, current], axis=1), jnp.concatenate([current, eye], axis=1)]
    )
    alpha_t = nt(eye, solved[:, total_cols:])
    inverse = inverse[:, total_cols:]
    alpha_own = nn(sel, alpha_t)
    others(
        zs,
        z,
        lambda s: z_copy(own_img.at[0], images.at[0], img_s.at[0], img_r.at[0], s, s).wait_recv(),
    )
    assemble(full_i, images.at[0])
    new = jnp.zeros((total_cols, total_cols), jnp.float32)
    for p in range(patches):
        r1 = full_r[p] - nn(alpha_t, full_i[p])
        full_d[p] = r1
        new = new + nt(r1, r1)
    new_out[:, 0:total_cols] = new
    news[c] = new_out[...]
    others(cells, c, lambda t: new_copy(t, c).start())
    for p in range(patches):
        own_res[p] = rhs[p] - nn(alpha_own, full_i[p])
        sol_out[p] = nn(alpha_own, full_r[p])
    others(cells, c, lambda s: new_copy(s, s).wait_recv())
    new = news[0]
    for k in range(1, cells):
        new = new + news[k]
    new = new[:, 0:total_cols]
    beta = nn(inverse, new)
    beta_t = nt(eye, beta)
    beta_own = nn(sel, beta_t)
    for p in range(patches):
        own_dir[p] = own_res[p] + nn(beta_own, full_r[p])
    halo_copy(1, own_dir, 0).start()
    halo_copy(1, own_dir, 1).start()
    cell_moment(1, own_dir)
    others(cells, c, lambda t: moment_copy(1, t, c).start())
    halo[1, pl.ds(patches, patches)] = own_dir[...]
    for p in range(patches):
        full_d[p] += nn(beta_t, full_r[p])

    apply_operator(1)
    others(zs, z, lambda t: z_copy(own_img.at[1], images.at[1], img_s.at[1], img_r.at[1], t, z).start())
    images[1, z] = own_img[1]
    share_strips(1, full_d, False)
    curve, _ = collect_strips(1)
    (solved,) = eliminate([jnp.concatenate([curve, new], axis=1)])
    alpha_t = nt(eye, solved[:, total_cols:])
    alpha_own = nn(sel, alpha_t)
    for p in range(patches):
        sol_out[p] += nn(alpha_own, full_d[p])
    others(
        zs,
        z,
        lambda s: z_copy(own_img.at[1], images.at[1], img_s.at[1], img_r.at[1], s, s).wait_recv(),
    )
    assemble(full_i, images.at[1])
    for p in range(patches):
        res_out[p] = own_res[p] - nn(alpha_own, full_i[p])

    for it in range(ITERS):
        halo_copy(it, own_dir, 0).wait_send()
        halo_copy(it, own_dir, 1).wait_send()
        others(cells, c, lambda t: moment_copy(it, t, c).wait_send())
        others(devices, me, lambda t: strip_copy(it, t, me).wait_send())
        others(
            zs,
            z,
            lambda t: z_copy(
                own_img.at[it], images.at[it], img_s.at[it], img_r.at[it], t, z
            ).wait_send(),
        )
    others(zs, z, lambda t: z_copy(rhs, gathered, gat_s, gat_r, t, z).wait_send())
    others(cells, c, lambda t: new_copy(t, c).wait_send())


def on_device(cells, zs, *args):
    rhs, near, neigh, up, su, far, tr, sd, dn = args
    patches, cols, width = rhs.shape
    full = cols * zs
    devices = cells * zs
    f32 = jnp.float32
    vmem = pl.BlockSpec(memory_space=pltpu.VMEM)
    smem = pl.BlockSpec(memory_space=pltpu.SMEM)
    hbm = pl.BlockSpec(memory_space=pl.ANY)
    dma = pltpu.SemaphoreType.DMA
    out = pl.pallas_call(
        functools.partial(kernel, cells, zs),
        out_shape=[jax.ShapeDtypeStruct(rhs.shape, f32)] * 2,
        in_specs=[vmem, hbm, smem, hbm, hbm, smem, hbm, hbm, hbm],
        out_specs=[vmem, vmem],
        scratch_shapes=[
            pltpu.VMEM(near.shape, near.dtype),
            pltpu.VMEM(up.shape, f32),
            pltpu.VMEM(su.shape, f32),
            pltpu.VMEM(tr.shape, f32),
            pltpu.VMEM(sd.shape, f32),
            pltpu.VMEM(dn.shape, f32),
            pltpu.VMEM((ITERS, 3 * patches, cols, width), f32),
            pltpu.VMEM((ITERS, cells, cols, 128), f32),
            pltpu.VMEM((ITERS, cols, 128), f32),
            pltpu.VMEM(rhs.shape, f32),
            pltpu.VMEM((ITERS,) + rhs.shape, f32),
            pltpu.VMEM(rhs.shape, f32),
            pltpu.VMEM((zs,) + rhs.shape, f32),
            pltpu.VMEM((ITERS, zs) + rhs.shape, f32),
            pltpu.VMEM((patches, full, width), f32),
            pltpu.VMEM((patches, full, width), f32),
            pltpu.VMEM((patches, full, width), f32),
            pltpu.VMEM((ITERS, 2, cols, 128), f32),
            pltpu.VMEM((ITERS, devices, 2, cols, 128), f32),
            pltpu.VMEM((full, 128), f32),
            pltpu.VMEM((cells, full, 128), f32),
            dma((patches,)),
            dma((5,)),
            dma((ITERS, 2)),
            dma((ITERS, 2)),
            dma((ITERS, cells)),
            dma((ITERS, cells)),
            dma((zs,)),
            dma((zs,)),
            dma((ITERS, zs)),
            dma((ITERS, zs)),
            dma((ITERS, devices)),
            dma((ITERS, devices)),
            dma((cells,)),
            dma((cells,)),
        ],
        compiler_params=pltpu.CompilerParams(
            collective_id=0, has_side_effects=True, vmem_limit_bytes=48 * 1024 * 1024
        ),
        name="block_cg",
    )(rhs, near, neigh, up, su, far, tr, sd, dn)
    return tuple(out)


def solution(mesh):
    cells = mesh.shape["patch"]
    zs = mesh.shape["rhs"]
    return jax.shard_map(
        functools.partial(on_device, cells, zs),
        mesh=mesh,
        in_specs=(
            P("patch", "rhs", None),
            P("patch", None, None, None),
            P("patch", None),
            P("patch", None, None),
            P("patch", None, None),
            P("patch", None),
            P("patch", None, None, None),
            P("patch", None, None),
            P("patch", None, None),
        ),
        out_specs=(P("patch", "rhs", None), P("patch", "rhs", None)),
        check_vma=False,
    )
```

time: 130 us -> 71.8 us (0.55)
  blocking collectives: 83.3 us -> 0 us
  Pallas kernels: 0 us -> 61.8 us
  matrix products: 27.2 us -> 0 us
  other arithmetic: 14.2 us -> 0 us
  local copies, waits for them, and re-layouts: 2.76 us -> 8.98 us
    pallas_call x0 -> x1, Pallas kernels: none -> 61.8 us  [on_device(): pl.pallas_call(functools.partial(kernel, cells, zs), out_shape=[jax.Shape...]
    psum x3 -> x0, blocking collectives: 49.2 us -> none  [the longest x2 35.7 us: residual_sum(): return lax.psum(gram(residual, residual), 'patch')]
    all_gather x3 -> x0, blocking collectives: 34.1 us -> none  [the longest x2 18.7 us: apply_operator(): piece = lax.all_gather(cell_moment[None], 'patch', axis=0, tiled=True)]
    dot_general x23 -> x0, matrix products: 26 us -> none  [the longest x2 12.5 us: apply_operator(): jnp.einsum('pjvw,pjkw->pkv', near_blocks, picked, preferred_element_type=...]
    another operation x15 -> x0, other arithmetic: 12 us -> none  [the longest x9 6.39 us: spd_solve(): factor = jnp.linalg.cholesky(matrix)]
    unnamed x13 -> x16, local copies, waits for them, and re-layouts: 0.93 us -> 8.98 us
  transfers between devices with their start and end apart: 4 -> 0, of which waited for: 0 -> 0; matrix products, arithmetic and copies ran while one was open for 8% -> 0% of each run, Pallas kernels for 0% -> 0%
where the time goes in v1:
time: 71.8 us; the launch traced here: 71.4 us
  Pallas kernels  61.8 us (86%)
  local copies, waits for them, and re-layouts  8.98 us (13%)
    pallas_call x1, Pallas kernels, on_device(): pl.pallas_call(functools.partial(kernel, cells, zs), out_shape=[jax.Shape...  61.8 us
    unnamed x16, local copies, waits for them, and re-layouts  8.98 us

profile of v1, /device:TPU:0, one launch (start us, length us, event | category | flops | bytes accessed | tf_op | source)
XLA Modules:
  0.0 71.4 jit_solution(923944249620117326)
XLA Ops:
  0.6 0.8 %copy.11.neigh = s32[8,4]{1,0:T(8,128)S(1)} copy(s32[8,4]{0,1:T(4,128)} %param.11) | data formatting | bytes 256 | tf_op args[2]
  1.4 1.6 %copy.12.dn_hbm = f32[8,384,64]{2,1,0:T(8,128)S(1)} copy(f32[8,384,64]{1,2,0:T(8,128)} %param.17) | data formatting | bytes 1572864 | tf_op args[8]
  3.0 0.0 copy-start
  3.0 1.1 %copy-done = f32[8,64,384]{2,1,0:T(8,128)S(1)} copy-done((f32[8,64,384]{2,1,0:T(8,128)S(1)}, f32[8,64,384]{2,1,0:T(8,128)}, u32[]{:S(2)}) %copy-start) | copy-done | bytes 786456
  4.1 0.0 copy-start.1
  4.1 0.9 %copy-done.1 = f32[8,64,64]{2,1,0:T(8,128)S(1)} copy-done((f32[8,64,64]{2,1,0:T(8,128)S(1)}, f32[8,64,64]{2,1,0:T(8,128)}, u32[]{:S(2)}) %copy-start.1) | copy-done | bytes 131096
  5.1 0.0 copy-start.2
  5.1 0.9 %copy-done.2 = f32[8,64,64]{2,1,0:T(8,128)S(1)} copy-done((f32[8,64,64]{2,1,0:T(8,128)S(1)}, f32[8,64,64]{2,1,0:T(8,128)}, u32[]{:S(2)}) %copy-start.2) | copy-done | bytes 131096
  6.0 0.0 copy-start.3
  6.0 0.9 %copy-done.3 = f32[1,4,64,64]{3,2,1,0:T(8,128)S(1)} copy-done((f32[1,4,64,64]{3,2,1,0:T(8,128)S(1)}, f32[1,4,64,64]{3,2,1,0:T(8,128)}, u32[]{:S(2)}) %copy-start.3) | copy-done | bytes 65560
  6.9 0.0 copy-start.4
  6.9 0.8 %copy-done.4 = f32[8,4,384]{2,1,0:T(4,128)S(1)} copy-done((f32[8,4,384]{2,1,0:T(4,128)S(1)}, f32[8,4,384]{2,1,0:T(4,128)}, u32[]{:S(2)}) %copy-start.4) | copy-done | bytes 49176
  7.7 0.0 copy-start.5
  7.7 0.7 copy-done.5
  8.4 61.8 %block_cg.1 = (f32[8,4,384]{2,1,0:T(4,128)S(1)}, f32[8,4,384]{2,1,0:T(4,128)S(1)}) custom-call(f32[8,4,384]{2,1,0:T(4,128)S(1)} %copy-done.4, bf16[8,4,384,384]{3,2,1,0:T(8,128)(2,1)} %near_hbm.1, s32[8,4]{1,0:T(8,128)S(1)} %copy.11.neigh, f32[8,64,384]{2,1,0:T(8,128)S(1)} %copy-done, f32[8,64,64]{2,1,0:T(8,128)S(1)} %copy-done.1, s32[1,4]{1,0:T(1,128)S(1)} %copy-done.5, ...), custom_call_target="tpu_custom_call" | custom-call | tf_op jit(solution)/shard_map/block_cg/pallas_call | solution.py:369
  70.2 0.6 copy.15
  70.8 0.6 copy.16
Async XLA Ops:
  3.0 1.1 %copy-start = (f32[8,64,384]{2,1,0:T(8,128)S(1)}, f32[8,64,384]{2,1,0:T(8,128)}, u32[]{:S(2)}) copy-start(f32[8,64,384]{2,1,0:T(8,128)} %up_hbm.1) | copy-start | bytes 2359300
  4.1 0.9 %copy-start.1 = (f32[8,64,64]{2,1,0:T(8,128)S(1)}, f32[8,64,64]{2,1,0:T(8,128)}, u32[]{:S(2)}) copy-start(f32[8,64,64]{2,1,0:T(8,128)} %su_hbm.1) | copy-start | bytes 393220
  5.1 0.9 %copy-start.2 = (f32[8,64,64]{2,1,0:T(8,128)S(1)}, f32[8,64,64]{2,1,0:T(8,128)}, u32[]{:S(2)}) copy-start(f32[8,64,64]{2,1,0:T(8,128)} %sd_hbm.1) | copy-start | bytes 393220
  6.0 0.9 %copy-start.3 = (f32[1,4,64,64]{3,2,1,0:T(8,128)S(1)}, f32[1,4,64,64]{3,2,1,0:T(8,128)}, u32[]{:S(2)}) copy-start(f32[1,4,64,64]{3,2,1,0:T(8,128)} %tr_hbm.1) | copy-start | bytes 196612
  6.9 0.8 %copy-start.4 = (f32[8,4,384]{2,1,0:T(4,128)S(1)}, f32[8,4,384]{2,1,0:T(4,128)}, u32[]{:S(2)}) copy-start(f32[8,4,384]{2,1,0:T(4,128)} %rhs.1) | copy-start | bytes 147460
  7.7 0.7 copy-start.5

commit v2 on v1

--- a/solution.py
+++ b/solution.py
@@ -22,6 +22,11 @@
     return lax.dot_general(
         a, b, (((1,), (0,)), ((), ())), precision=HIGH, preferred_element_type=jnp.float32
     )
+
+
+def split(x):
+    high = x.astype(jnp.bfloat16)
+    return high, (x - high.astype(jnp.float32)).astype(jnp.bfloat16)
 
 
 def eliminate(systems):
@@ -56,6 +61,8 @@
     tr,
     sd,
     dn,
+    gcat,
+    ucat,
     halo,
     moment,
     mom_out,
@@ -202,26 +209,28 @@
             if it == 0:
                 near_copy(p).wait()
             acc = jnp.zeros((cols, width), jnp.float32)
-            for j in range(neigh.shape[1]):
+            for j in range(neigh.shape[0]):
                 if j == 0:
                     x = halo[it, patches + p]
                 else:
-                    spot = jnp.minimum(lax.rem(neigh[p, j] - first + total, total), 3 * patches - 1)
+                    spot = jnp.minimum(lax.rem(neigh[j, p] - first + total, total), 3 * patches - 1)
                     x = halo[it, spot]
                 acc = acc + nt(x.astype(jnp.bfloat16), blocks[p, j], None)
             own_img[it, p] = acc
             return carry
 
-        lax.fori_loop(0, patches, near, 0)
+        for p in range(patches):
+            near(p, 0)
         others(cells, c, lambda s: moment_copy(it, s, s).wait_recv())
-        if it == 0:
-            for copy in map_copies[2:]:
-                copy.wait()
         local = jnp.zeros((cols, terms), jnp.float32)
         for j in range(far.shape[1]):
             local = local + nt(moment[it, far[0, j]][:, 0:terms], tr[0, j])
-        for p in range(patches):
-            own_img[it, p] += nt(nt(local, sd[p]), dn[p])
+        high, low = split(local)
+        local = jnp.concatenate(
+            [high.astype(jnp.float32), high.astype(jnp.float32), low.astype(jnp.float32)], axis=1
+        ).astype(jnp.bfloat16)
+        for p in range(patches):
+            own_img[it, p] += jnp.dot(local, gcat[p], preferred_element_type=jnp.float32)
 
     def assemble(full, buf):
         for p in range(patches):
@@ -239,6 +248,37 @@
     others(cells, c, lambda t: moment_copy(0, t, c).start())
     others(zs, z, lambda t: z_copy(rhs, gathered, gat_s, gat_r, t, z).start())
 
+    for copy in map_copies[2:]:
+        copy.wait()
+    for p in range(patches):
+        both = lax.dot_general(
+            sd[p],
+            dn[p],
+            (((0,), (0,)), ((), ())),
+            precision=HIGH,
+            preferred_element_type=jnp.float32,
+        )
+        high, low = split(both)
+        gcat[p, 0:terms, :] = high
+        gcat[p, terms : 2 * terms, :] = low
+        gcat[p, 2 * terms : 3 * terms, :] = high
+
+    def combine_up():
+        for p in range(patches):
+            high, low = split(nn(su[p], up[p]))
+            ucat[p, 0:terms, :] = high
+            ucat[p, terms : 2 * terms, :] = low
+
+    def later_moment(it, src):
+        acc = jnp.zeros((2 * cols, 2 * terms), jnp.float32)
+        for p in range(patches):
+            high, low = split(src[p])
+            x = jnp.concatenate([high.astype(jnp.float32), low.astype(jnp.float32)], axis=0)
+            acc = acc + nt(x.astype(jnp.bfloat16), ucat[p], None)
+        acc = acc[:, 0:terms] + acc[:, terms:]
+        mom_out[it, :, :] = jnp.zeros(mom_out.shape[1:], jnp.float32)
+        mom_out[it, :, 0:terms] = acc[0:cols] + acc[cols:]
+
     sel = (
         lax.broadcasted_iota(jnp.int32, (cols, total_cols), 1)
         == lax.broadcasted_iota(jnp.int32, (cols, total_cols), 0) + z * cols
@@ -249,14 +289,15 @@
     ).astype(jnp.float32)
 
     def share_strips(it, direction, with_rr):
-        acc = jnp.zeros((cols, total_cols), jnp.float32)
-        cur = jnp.zeros((cols, total_cols), jnp.float32)
-        for p in range(patches):
-            acc = acc + nt(own_img[it, p], direction[p])
+        acc = jnp.zeros(((2 if with_rr else 1) * cols, total_cols), jnp.float32)
+        for p in range(patches):
+            left = own_img[it, p]
             if with_rr:
-                cur = cur + nt(rhs[p], direction[p])
-        strip_out[it, 0, :, 0:total_cols] = acc
-        strip_out[it, 1, :, 0:total_cols] = cur
+                left = jnp.concatenate([left, rhs[p]], axis=0)
+            acc = acc + nt(left, direction[p])
+        if with_rr:
+            acc = jnp.concatenate([acc[0:cols], acc[cols:]], axis=1)
+        strip_out[it, :, 0 : acc.shape[1]] = acc
         strips[it, me] = strip_out[it]
         others(devices, me, lambda t: strip_copy(it, t, me).start())
 
@@ -267,18 +308,19 @@
             acc = strips[it, s]
             for k in range(1, cells):
                 acc = acc + strips[it, k * zs + s]
-            curve.append(acc[0, :, 0:total_cols])
-            cur.append(acc[1, :, 0:total_cols])
+            curve.append(acc[:, 0:total_cols])
+            cur.append(acc[:, total_cols : 2 * total_cols])
         curve = jnp.concatenate(curve, axis=0)
         cur = jnp.concatenate(cur, axis=0)
         return 0.5 * (curve + nt(eye, curve)), cur
 
     apply_operator(0)
-    others(zs, z, lambda t: z_copy(own_img.at[0], images.at[0], img_s.at[0], img_r.at[0], t, z).start())
-    images[0, z] = own_img[0]
     others(zs, z, lambda s: z_copy(rhs, gathered, gat_s, gat_r, s, s).wait_recv())
     assemble(full_r, gathered)
     share_strips(0, full_r, True)
+    others(zs, z, lambda t: z_copy(own_img.at[0], images.at[0], img_s.at[0], img_r.at[0], t, z).start())
+    images[0, z] = own_img[0]
+    combine_up()
     curve, current = collect_strips(0)
     solved, inverse = eliminate(
         [jnp.concatenate([curve, current], axis=1), jnp.concatenate([current, eye], axis=1)]
@@ -315,16 +357,16 @@
         own_dir[p] = own_res[p] + nn(beta_own, full_r[p])
     halo_copy(1, own_dir, 0).start()
     halo_copy(1, own_dir, 1).start()
-    cell_moment(1, own_dir)
+    later_moment(1, own_dir)
     others(cells, c, lambda t: moment_copy(1, t, c).start())
     halo[1, pl.ds(patches, patches)] = own_dir[...]
     for p in range(patches):
         full_d[p] += nn(beta_t, full_r[p])
 
     apply_operator(1)
+    share_strips(1, full_d, False)
     others(zs, z, lambda t: z_copy(own_img.at[1], images.at[1], img_s.at[1], img_r.at[1], t, z).start())
     images[1, z] = own_img[1]
-    share_strips(1, full_d, False)
     curve, _ = collect_strips(1)
     (solved,) = eliminate([jnp.concatenate([curve, new], axis=1)])
     alpha_t = nt(eye, solved[:, total_cols:])
@@ -359,6 +401,8 @@
 def on_device(cells, zs, *args):
     rhs, near, neigh, up, su, far, tr, sd, dn = args
     patches, cols, width = rhs.shape
+    dn = jnp.swapaxes(dn, 1, 2)
+    neigh = neigh.T
     full = cols * zs
     devices = cells * zs
     f32 = jnp.float32
@@ -378,6 +422,8 @@
             pltpu.VMEM(tr.shape, f32),
             pltpu.VMEM(sd.shape, f32),
             pltpu.VMEM(dn.shape, f32),
+            pltpu.VMEM((patches, 3 * su.shape[1], width), jnp.bfloat16),
+            pltpu.VMEM((patches, 2 * su.shape[1], width), jnp.bfloat16),
             pltpu.VMEM((ITERS, 3 * patches, cols, width), f32),
             pltpu.VMEM((ITERS, cells, cols, 128), f32),
             pltpu.VMEM((ITERS, cols, 128), f32),
@@ -389,8 +435,8 @@
             pltpu.VMEM((patches, full, width), f32),
             pltpu.VMEM((patches, full, width), f32),
             pltpu.VMEM((patches, full, width), f32),
-            pltpu.VMEM((ITERS, 2, cols, 128), f32),
-            pltpu.VMEM((ITERS, devices, 2, cols, 128), f32),
+            pltpu.VMEM((ITERS, cols, 128), f32),
+            pltpu.VMEM((ITERS, devices, cols, 128), f32),
             pltpu.VMEM((full, 128), f32),
             pltpu.VMEM((cells, full, 128), f32),
             dma((patches,)),
@@ -409,7 +455,7 @@
             dma((cells,)),
         ],
         compiler_params=pltpu.CompilerParams(
-            collective_id=0, has_side_effects=True, vmem_limit_bytes=48 * 1024 * 1024
+            collective_id=0, has_side_effects=True, vmem_limit_bytes=60 * 1024 * 1024
         ),
         name="block_cg",
     )(rhs, near, neigh, up, su, far, tr, sd, dn)

time: 71.8 us -> 53.8 us (0.75)
  Pallas kernels: 61.8 us -> 50.1 us
  local copies, waits for them, and re-layouts: 8.98 us -> 2.85 us
    pallas_call x1, Pallas kernels: 61.8 us -> 50.1 us  [on_device(): pl.pallas_call(functools.partial(kernel, cells, zs), out_shape=[jax.Shape...]
    unnamed x16 -> x2, local copies, waits for them, and re-layouts: 8.98 us -> 2.85 us
where the time goes in v2:
time: 53.8 us; the launch traced here: 53.5 us
  Pallas kernels  50.1 us (93%)
  local copies, waits for them, and re-layouts  2.85 us (5%)
  between operations  0.64 us (1%)
    pallas_call x1, Pallas kernels, on_device(): pl.pallas_call(functools.partial(kernel, cells, zs), out_shape=[jax.Shape...  50.1 us
    unnamed x2, local copies, waits for them, and re-layouts  2.85 us

profile of v2, /device:TPU:0, one launch (start us, length us, event | category | flops | bytes accessed | tf_op | source)
XLA Modules:
  0.0 53.5 jit_solution(14740106246872070696)
XLA Ops:
  0.6 50.1 %block_cg.1 = (f32[8,4,384]{2,1,0:T(4,128)}, f32[8,4,384]{2,1,0:T(4,128)}) custom-call(f32[8,4,384]{2,1,0:T(4,128)} %rhs.1, bf16[8,4,384,384]{3,2,1,0:T(8,128)(2,1)} %near_hbm.1, s32[4,8]{1,0:T(4,128)} %bitcast.3, f32[8,64,384]{2,1,0:T(8,128)} %up_hbm.1, f32[8,64,64]{2,1,0:T(8,128)} %su_hbm.1, s32[1,4]{1,0:T(1,128)} %far.1, f32[1,4,64,64]{3,2,1,0:T(8,128)} %tr_hbm.1, ...), custom_call_target="tpu_custom_call" | custom-call | tf_op jit(solution)/shard_map/block_cg/pallas_call | solution.py:413
  50.7 1.4 %copy.13 = f32[8,4,384]{2,1,0:T(4,128)} copy(f32[8,4,384]{2,1,0:T(4,128)} %get-tuple-element.4) | data formatting | bytes 98304
  52.1 1.4 %copy.14 = f32[8,4,384]{2,1,0:T(4,128)} copy(f32[8,4,384]{2,1,0:T(4,128)} %get-tuple-element.5) | data formatting | bytes 98304
